TPU v7x, 32 devices: a whole 2x2x4 slice. The times are simulated.
32 devices in a mesh: gx: 4 (over x, core), gy: 2 (over y), gz: 4 (over z).
Axes of the slice: x: 2, y: 2, z: 4, core: 2. Of those that a mesh axis runs over, the one named last changes fastest.
Arguments:
- warped_image: float32 [256, 128, 512], P('gx', 'gy', 'gz'), may hold values from -6 to 6
- fixed_image: float32 [256, 128, 512], P('gx', 'gy', 'gz'), may hold values from -6 to 6
- fine_control: float32 [3, 32, 16, 64], P(None, 'gx', 'gy', 'gz'), may hold values from -6 to 6
- coarse_control: float32 [3, 8, 4, 16], replicated, may hold values from -6 to 6
Outputs:
- fine_gradient: float32 [3, 32, 16, 64], P(None, 'gx', 'gy', 'gz')
- coarse_gradient: float32 [3, 8, 4, 16], replicated
All inputs are finite; a program needn't handle non-finite values.
Results may differ from a plain program's by a relative error of at most 0.0003.
Values sent between devices are 32-bit elements; how exact they have to be, the bound alone decides.
A program may use at most 64 MiB of HBM per device.

v0:
```python
import jax
import jax.numpy as jnp
from jax import lax
from jax.sharding import PartitionSpec as P

SPF = 8
SPC = 32
bend_factor = 0.01
highest = lax.Precision.HIGHEST


def padded_2(block, sides, width):
    for axis, dim in sides:
        count = lax.axis_size(axis)
        forward = [(i, i + 1) for i in range(count - 1)]
        backward = [(target, source) for source, target in forward]
        low = lax.ppermute(
            lax.slice_in_dim(block, block.shape[dim] - width, None, axis=dim), axis, forward
        )
        high = lax.ppermute(lax.slice_in_dim(block, 0, width, axis=dim), axis, backward)
        block = jnp.concatenate([low, block, high], axis=dim)
    return block


def spline(values):
    magnitude = jnp.abs(values)
    inner = 2.0 / 3.0 - magnitude * magnitude + 0.5 * magnitude * magnitude * magnitude
    remain = 2.0 - magnitude
    outer = remain * remain * remain / 6.0
    return jnp.where(magnitude < 1.0, inner, jnp.where(magnitude < 2.0, outer, 0.0 * magnitude))


def basis_matrix(voxels, points, spacing, voxel_start, point_start):
    voxel = (jnp.arange(voxels, dtype=jnp.int32) + voxel_start).astype(jnp.float32) + 0.5
    centre = (jnp.arange(points, dtype=jnp.int32) + point_start).astype(
        jnp.float32
    ) * spacing + 0.5 * spacing
    return spline((voxel[:, None] - centre[None, :]) / spacing)


def slope(padded, axis):
    rank = padded.ndim
    count = padded.shape[axis] - 4

    def shifted(offset):
        piece = lax.slice_in_dim(padded, offset, offset + count, axis=axis)
        for other in range(rank - 3, rank):
            if other != axis:
                piece = lax.slice_in_dim(piece, 2, piece.shape[other] - 2, axis=other)
        return piece

    return (shifted(0) - 8.0 * shifted(1) + 8.0 * shifted(3) - shifted(4)) / 12.0


def stencil(padded):
    centre = padded[:, 1:-1, 1:-1, 1:-1]
    total = padded[:, 2:, 1:-1, 1:-1] + padded[:, :-2, 1:-1, 1:-1]
    total = total + padded[:, 1:-1, 2:, 1:-1] + padded[:, 1:-1, :-2, 1:-1]
    total = total + padded[:, 1:-1, 1:-1, 2:] + padded[:, 1:-1, 1:-1, :-2]
    return total - 6.0 * centre


def laplace(field):
    return stencil(jnp.pad(field, ((0, 0), (1, 1), (1, 1), (1, 1))))


def project(force, along_x, along_y, along_z):
    section = jnp.einsum("axyz,xp->apyz", force, along_x, precision=highest)
    section = jnp.einsum("apyz,yq->apqz", section, along_y, precision=highest)
    return jnp.einsum("apqz,zr->apqr", section, along_z, precision=highest)


def settle(extended, axis, points):
    own_part = lax.slice_in_dim(extended, 4, points + 4, axis=axis)
    from_left = lax.slice_in_dim(extended, 0, 2, axis=axis)
    from_right = lax.slice_in_dim(extended, points + 6, points + 8, axis=axis)
    leading = [(0, 0)] * extended.ndim
    trailing = [(0, 0)] * extended.ndim
    leading[axis] = (0, points - 2)
    trailing[axis] = (points - 2, 0)
    return own_part + jnp.pad(from_left, leading) + jnp.pad(from_right, trailing)


def inside(position, points, devices):
    global_index = position * points - 1 + jnp.arange(points + 2, dtype=jnp.int32)
    return ((global_index >= 0) & (global_index < points * devices)).astype(jnp.float32)


def per_device(warped_image, fixed_image, fine_control, coarse_control):
    size_x, size_y, size_z = warped_image.shape
    difference = warped_image - fixed_image
    padded = padded_2(warped_image + fixed_image, (("gx", 0), ("gy", 1), ("gz", 2)), 2)
    slopes = [0.5 * slope(padded, axis) for axis in range(3)]
    force = jnp.stack(slopes) * difference[None]
    points_x = size_x // SPF
    points_y = size_y // SPF
    points_z = size_z // SPF
    part = project(
        force,
        basis_matrix(size_x, points_x + 4, SPF, 0, -2),
        basis_matrix(size_y, points_y + 4, SPF, 0, -2),
        basis_matrix(size_z, points_z + 4, SPF, 0, -2),
    )
    part = settle(padded_2(part, (("gx", 1),), 2), 1, points_x)
    part = settle(padded_2(part, (("gy", 2),), 2), 2, points_y)
    part = settle(padded_2(part, (("gz", 3),), 2), 3, points_z)
    control = padded_2(fine_control, (("gx", 1), ("gy", 2), ("gz", 3)), 2)
    first = stencil(control)
    valid_x = inside(lax.axis_index("gx"), points_x, lax.axis_size("gx"))
    valid_y = inside(lax.axis_index("gy"), points_y, lax.axis_size("gy"))
    valid_z = inside(lax.axis_index("gz"), points_z, lax.axis_size("gz"))
    region = valid_x[:, None, None] * valid_y[None, :, None] * valid_z[None, None, :]
    first = first * region[None]
    fine_gradient = part * SPF ** (-1.5) + bend_factor * stencil(first)
    coarse_x = basis_matrix(size_x, coarse_control.shape[1], SPC, lax.axis_index("gx") * size_x, 0)
    coarse_y = basis_matrix(size_y, coarse_control.shape[2], SPC, lax.axis_index("gy") * size_y, 0)
    coarse_z = basis_matrix(size_z, coarse_control.shape[3], SPC, lax.axis_index("gz") * size_z, 0)
    coarse_part = project(force, coarse_x, coarse_y, coarse_z)
    coarse_sum = lax.psum(coarse_part, ("gx", "gy", "gz"))
    coarse_gradient = coarse_sum * SPC ** (-1.5) + bend_factor * laplace(laplace(coarse_control))
    return (fine_gradient, coarse_gradient)


def solution(mesh):
    in_specs = (P("gx", "gy", "gz"), P("gx", "gy", "gz"), P(None, "gx", "gy", "gz"), P())
    out_specs = (P(None, "gx", "gy", "gz"), P())
    return jax.shard_map(
        per_device, mesh=mesh, in_specs=in_specs, out_specs=out_specs, check_vma=False
    )
```

profile of v0, /device:TPU:0, one launch (start us, length us, event | category | flops | bytes accessed | tf_op | source)
XLA Modules:
  0.0 158.9 jit_solution(8543917966219928136)
XLA Ops:
  0.7 4.4 %fusion.237 = (f32[64,64,128]{2,1,0:T(8,128)}, f32[64,64,128]{2,1,0:T(8,128)S(1)}) fusion(f32[64,64,128]{2,1,0:T(8,128)} %param.4, f32[64,64,128]{2,1,0:T(8,128)} %param.5), kind=kLoop, calls=%fused_computation.303 | loop fusion | flops 1048576 | bytes 8388608 | tf_op jit(solution)/shard_map/sub | solution.py:91
  5.1 2.4 %collective-permute-start = (f32[2,64,128]{2,1,0:T(8,128)S(1)}, f32[2,64,128]{2,1,0:T(8,128)S(1)}, u32[]{:S(2)}, u32[]{:S(2)}) collective-permute-start(f32[2,64,128]{2,1,0:T(8,128)S(1)} %get-tuple-element.16), channel_id=1, source_target_pairs={{0,8},{8,16},{16,24},{1,9},{9,17},{17,25},{2,10},{10,18},{18,26},{... | collective-permute-start | bytes 196616 | tf_op jit(solution)/shard_map/ppermute | solution.py:17
  7.5 1.3 collective-permute-start.1
  8.8 5.1 %collective-permute-start.12 = (f32[3,2,8,16]{3,2,1,0:T(8,128)S(1)}, f32[3,2,8,16]{3,2,1,0:T(8,128)S(1)}, u32[]{:S(2)}, u32[]{:S(2)}) collective-permute-start(f32[3,2,8,16]{3,2,1,0:T(8,128)S(1)} %get-tuple-element.29), channel_id=1, source_target_pairs={{0,8},{8,16},{16,24},{1,9},{9,17},{17,25},{2,10},{10,18},{18,26},{... | collective-permute-start | bytes 9224 | tf_op jit(solution)/shard_map/ppermute | solution.py:17
  14.0 1.3 collective-permute-start.13
  15.4 0.1 fusion.51
  15.5 0.1 broadcast_multiply_fusion.1
  15.6 0.1 broadcast_multiply_fusion
  15.7 0.0 collective-permute-done.12
  15.7 2.6 %collective-permute-done.13 = f32[3,2,8,16]{3,2,1,0:T(8,128)S(1)} collective-permute-done((f32[3,2,8,16]{3,2,1,0:T(8,128)S(1)}, f32[3,2,8,16]{3,2,1,0:T(8,128)S(1)}, u32[]{:S(2)}, u32[]{:S(2)}) %collective-permute-start.13) | collective-permute-done | bytes 3104 | tf_op jit(solution)/shard_map/ppermute | solution.py:20
  18.3 3.4 %collective-permute-start.14 = (f32[3,12,2,16]{3,2,1,0:T(2,128)S(1)}, f32[3,12,2,16]{3,2,1,0:T(2,128)S(1)}, u32[]{:S(2)}, u32[]{:S(2)}) collective-permute-start(f32[3,12,2,16]{3,2,1,0:T(2,128)S(1)} %get-tuple-element.24), channel_id=1, source_target_pairs={{0,4},{1,5},{2,6},{3,7},{8,12},{9,13},{10,14},{11,15},{16,20},{17,... | collective-permute-start | bytes 13832 | tf_op jit(solution)/shard_map/ppermute | solution.py:17
  21.8 1.3 collective-permute-start.15
  23.1 0.3 collective-permute-done.14
  23.4 4.2 %collective-permute-done.15 = f32[3,12,2,16]{3,2,1,0:T(2,128)S(1)} collective-permute-done((f32[3,12,2,16]{3,2,1,0:T(2,128)S(1)}, f32[3,12,2,16]{3,2,1,0:T(2,128)S(1)}, u32[]{:S(2)}, u32[]{:S(2)}) %collective-permute-start.15) | collective-permute-done | bytes 4640 | tf_op jit(solution)/shard_map/ppermute | solution.py:20
  27.6 0.1 pad_maximum_fusion.14
  27.7 0.1 fusion.241
  27.8 3.5 %collective-permute-start.16 = (f32[3,12,12,2]{3,2,1,0:T(8,128)S(1)}, f32[3,12,12,2]{3,2,1,0:T(8,128)S(1)}, u32[]{:S(2)}, u32[]{:S(2)}) collective-permute-start(f32[3,12,12,2]{3,2,1,0:T(8,128)S(1)} %get-tuple-element.20), channel_id=1, source_target_pairs={{0,1},{1,2},{2,3},{4,5},{5,6},{6,7},{8,9},{9,10},{10,11},{12,13},{... | collective-permute-start | bytes 10376 | tf_op jit(solution)/shard_map/ppermute | solution.py:17
  31.3 1.3 collective-permute-start.17
  32.7 5.9 %collective-permute-done.16 = f32[3,12,12,2]{3,2,1,0:T(8,128)S(1)} collective-permute-done((f32[3,12,12,2]{3,2,1,0:T(8,128)S(1)}, f32[3,12,12,2]{3,2,1,0:T(8,128)S(1)}, u32[]{:S(2)}, u32[]{:S(2)}) %collective-permute-start.16) | collective-permute-done | bytes 3488 | tf_op jit(solution)/shard_map/ppermute | solution.py:17
  38.5 4.4 %collective-permute-done.17 = f32[3,12,12,2]{3,2,1,0:T(8,128)S(1)} collective-permute-done((f32[3,12,12,2]{3,2,1,0:T(8,128)S(1)}, f32[3,12,12,2]{3,2,1,0:T(8,128)S(1)}, u32[]{:S(2)}, u32[]{:S(2)}) %collective-permute-start.17) | collective-permute-done | bytes 3488 | tf_op jit(solution)/shard_map/ppermute | solution.py:20
  43.0 0.3 pad_maximum_fusion.15
  43.3 0.6 fusion.36
  43.9 0.0 collective-permute-done
  43.9 0.0 collective-permute-done.1
  43.9 0.1 pad_maximum_fusion.24
  44.0 1.6 collective-permute-start.2
  45.5 1.3 collective-permute-start.3
  46.8 2.2 %fusion.9 = f32[1,64,64,128]{3,2,1,0:T(8,128)} fusion(f32[64,64,128]{2,1,0:T(8,128)S(1)} %get-tuple-element.9, f32[2,64,128]{2,1,0:T(8,128)S(1)} %collective-permute-done.1, f32[2,64,128]{2,1,0:T(8,128)S(1)} %collective-permute-done), kind=kLoop, calls=%fused_computation.17 | loop fusion | flops 5242880 | bytes 4325376 | tf_op jit(solution)/shard_map/stack | solution.py:94
  49.0 0.0 collective-permute-done.2
  49.0 2.7 %collective-permute-done.3 = f32[68,2,128]{2,1,0:T(2,128)S(1)} collective-permute-done((f32[68,2,128]{2,1,0:T(2,128)S(1)}, f32[68,2,128]{2,1,0:T(2,128)S(1)}, u32[]{:S(2)}, u32[]{:S(2)}) %collective-permute-start.3) | collective-permute-done | bytes 69664 | tf_op jit(solution)/shard_map/ppermute | solution.py:20
  51.7 0.4 pad_maximum_fusion.1
  52.1 3.0 %fusion.238 = (f32[68,68,2]{2,1,0:T(8,128)}, f32[68,68,2]{2,1,0:T(8,128)}) fusion(f32[68,68,128]{2,1,0:T(8,128)S(1)} %pad_maximum_fusion.1), kind=kLoop, calls=%fused_computation.304 | loop fusion | bytes 147968 | tf_op jit(solution)/shard_map/slice | solution.py:18
  55.1 2.6 %copy.19 = f32[68,68,2]{1,0,2:T(8,128)S(1)} copy(f32[68,68,2]{2,1,0:T(8,128)} %get-tuple-element.11) | data formatting | bytes 73984 | tf_op jit(solution)/shard_map/slice | solution.py:20
  57.7 1.3 collective-permute-start.5
  59.0 2.6 %copy.17 = f32[68,68,2]{1,2,0:T(2,128)S(1)} copy(f32[68,68,2]{2,1,0:T(8,128)} %get-tuple-element.10) | data formatting | bytes 73984 | tf_op jit(solution)/shard_map/slice | solution.py:18
  61.6 4.6 %collective-permute-start.4 = (f32[68,68,2]{1,2,0:T(2,128)S(1)}, f32[68,68,2]{1,2,0:T(2,128)S(1)}, u32[]{:S(2)}, u32[]{:S(2)}) collective-permute-start(f32[68,68,2]{1,2,0:T(2,128)S(1)} %copy.17), channel_id=1, source_target_pairs={{0,1},{1,2},{2,3},{4,5},{5,6},{6,7},{8,9},{9,10},{10,11},{12,13},{... | collective-permute-start | bytes 110984 | tf_op jit(solution)/shard_map/ppermute | solution.py:17
  66.2 0.4 maximum_maximum_fusion
  66.6 2.1 %fusion.19 = f32[1,64,64,128]{3,2,1,0:T(8,128)} fusion(f32[68,66,128]{2,1,0:T(8,128)S(1)} %get-tuple-element.13, f32[68,66,128]{2,1,0:T(8,128)S(1)} %get-tuple-element.12), kind=kLoop, calls=%fused_computation.39 | loop fusion | flops 3145728 | bytes 10485760 | tf_op jit(solution)/shard_map/stack | solution.py:94
  68.8 0.0 collective-permute-done.5
  68.8 2.4 %copy.20 = f32[68,68,2]{2,1,0:T(8,128)} copy(f32[68,68,2]{1,0,2:T(8,128)S(1)} %collective-permute-done.5) | data formatting | bytes 73984 | tf_op jit(solution)/shard_map/ppermute | solution.py:20
  71.1 0.0 collective-permute-done.4
  71.1 2.4 %copy.18 = f32[68,68,2]{2,1,0:T(8,128)} copy(f32[68,68,2]{1,2,0:T(2,128)S(1)} %collective-permute-done.4) | data formatting | bytes 73984 | tf_op jit(solution)/shard_map/ppermute | solution.py:17
  73.5 10.4 %fusion.14 = f32[1,64,64,128]{3,2,1,0:T(8,128)S(1)} fusion(f32[68,68,2]{2,1,0:T(8,128)} %copy.20, f32[68,2,128]{2,1,0:T(2,128)S(1)} %collective-permute-done.3, f32[68,2,128]{2,1,0:T(2,128)S(1)} %collective-permute-done.2, f32[2,64,128]{2,1,0:T(8,128)S(1)} %collective-permute-done.1, f32[64,64,128]{2,1,0:T(8,128)S(1)} %get-tuple-element.9, ...), kind=kLoop, calls=%fused_computation.23 | loop fusion | flops 13631488 | bytes 4538624 | tf_op jit(solution)/shard_map/stack | solution.py:94
  83.9 1.1 maximum_multiply_fusion
  85.0 6.5 %fusion.23 = f32[3,12,64,128]{3,1,2,0:T(8,128)S(1)} fusion(f32[3,64,64,128]{3,2,1,0:T(8,128)S(1)} %maximum_multiply_fusion, f32[12]{0:T(128)S(1)} %multiply_add_fusion.4, f32[64]{0:T(128)S(1)} %convert_add_fusion.4), kind=kOutput, calls=%fused_computation.47 | convolution fusion | flops 226506240 | bytes 7471408 | tf_op jit(solution)/shard_map/axyz,xp->apyz/dot_general | solution.py:68
  91.4 1.0 fusion.31
  92.4 0.5 fusion.65
  92.9 1.3 collective-permute-start.6
  94.2 1.5 collective-permute-start.7
  95.7 6.5 %fusion.26 = f32[3,8,64,128]{3,1,2,0:T(8,128)S(1)} fusion(f32[3,64,64,128]{3,2,1,0:T(8,128)S(1)} %maximum_multiply_fusion, f32[8]{0:T(128)S(1)} %multiply_add_fusion.1, f32[64]{0:T(128)S(1)} %convert_add_fusion.1), kind=kOutput, calls=%fused_computation.48 | convolution fusion | flops 151004160 | bytes 7078176 | tf_op jit(solution)/shard_map/axyz,xp->apyz/dot_general | solution.py:68
  102.2 0.6 convolution_bitcast_fusion
  102.8 0.0 collective-permute-done.7
  102.9 1.8 %collective-permute-start.8 = (f32[3,8,2,20]{3,2,1,0:T(2,128)S(1)}, f32[3,8,2,20]{3,2,1,0:T(2,128)S(1)}, u32[]{:S(2)}, u32[]{:S(2)}) collective-permute-start(f32[3,8,2,20]{3,2,1,0:T(2,128)S(1)} %get-tuple-element.22), channel_id=1, source_target_pairs={{0,4},{1,5},{2,6},{3,7},{8,12},{9,13},{10,14},{11,15},{16,20},{17,... | collective-permute-start | bytes 11528 | tf_op jit(solution)/shard_map/ppermute | solution.py:17
  104.7 1.3 collective-permute-start.9
  106.0 0.2 fusion.60
  106.2 42.9 %psum.7 = f32[3,8,4,16]{3,1,2,0:T(8,128)S(1)} all-reduce(f32[3,8,4,16]{3,1,2,0:T(8,128)S(1)} %fusion.60), channel_id=1, replica_groups=mesh['gx'=4,'gy'=2,'gz'=4] {'gx','gy','gz'}, use_global_device_ids=true, to_apply=%region_0.1 | all-reduce | flops 1536 | bytes 12288 | tf_op jit(solution)/shard_map/psum | solution.py:119
  149.2 0.1 fusion.244
  149.3 2.2 %collective-permute-start.10 = (f32[3,8,8,2]{3,2,1,0:T(8,128)S(1)}, f32[3,8,8,2]{3,2,1,0:T(8,128)S(1)}, u32[]{:S(2)}, u32[]{:S(2)}) collective-permute-start(f32[3,8,8,2]{3,2,1,0:T(8,128)S(1)} %get-tuple-element.26), channel_id=1, source_target_pairs={{0,1},{1,2},{2,3},{4,5},{5,6},{6,7},{8,9},{9,10},{10,11},{12,13},{... | collective-permute-start | bytes 4616 | tf_op jit(solution)/shard_map/ppermute | solution.py:17
  151.5 1.3 collective-permute-start.11
  152.8 0.1 fusion.59
  152.9 0.6 copy.28
  153.5 0.2 collective-permute-done.10
  153.7 4.3 %collective-permute-done.11 = f32[3,8,8,2]{3,2,1,0:T(8,128)S(1)} collective-permute-done((f32[3,8,8,2]{3,2,1,0:T(8,128)S(1)}, f32[3,8,8,2]{3,2,1,0:T(8,128)S(1)}, u32[]{:S(2)}, u32[]{:S(2)}) %collective-permute-start.11) | collective-permute-done | bytes 1568 | tf_op jit(solution)/shard_map/ppermute | solution.py:20
  158.0 0.9 fusion.42
  (36 shorter events, 0.3 us)
Async XLA Ops:
  0.6 8.2 %copy-start.3 = (f32[3,8,8,16]{3,2,1,0:T(8,128)S(1)}, f32[3,8,8,16]{3,2,1,0:T(8,128)}, u32[]{:S(2)}) copy-start(f32[3,8,8,16]{3,2,1,0:T(8,128)} %param.6) | copy-start | bytes 36868
  0.6 14.7 %copy-start.4 = (f32[3,8,4,16]{3,2,1,0:T(4,128)S(1)}, f32[3,8,4,16]{3,2,1,0:T(4,128)}, u32[]{:S(2)}) copy-start(f32[3,8,4,16]{3,2,1,0:T(4,128)} %param.7) | copy-start | bytes 18436
  5.1 38.8 %collective-permute-start = (f32[2,64,128]{2,1,0:T(8,128)S(1)}, f32[2,64,128]{2,1,0:T(8,128)S(1)}, u32[]{:S(2)}, u32[]{:S(2)}) collective-permute-start(f32[2,64,128]{2,1,0:T(8,128)S(1)} %get-tuple-element.16), channel_id=1, source_target_pairs={{0,8},{8,16},{16,24},{1,9},{9,17},{17,25},{2,10},{10,18},{18,26},{... | collective-permute-start | bytes 196616 | tf_op jit(solution)/shard_map/ppermute | solution.py:17
  7.5 36.4 %collective-permute-start.1 = (f32[2,64,128]{2,1,0:T(8,128)S(1)}, f32[2,64,128]{2,1,0:T(8,128)S(1)}, u32[]{:S(2)}, u32[]{:S(2)}) collective-permute-start(f32[2,64,128]{2,1,0:T(8,128)S(1)} %get-tuple-element.17), channel_id=1, source_target_pairs={{8,0},{16,8},{24,16},{9,1},{17,9},{25,17},{10,2},{18,10},{26,18},{... | collective-permute-start | bytes 196616 | tf_op jit(solution)/shard_map/ppermute | solution.py:20
  8.8 6.9 %collective-permute-start.12 = (f32[3,2,8,16]{3,2,1,0:T(8,128)S(1)}, f32[3,2,8,16]{3,2,1,0:T(8,128)S(1)}, u32[]{:S(2)}, u32[]{:S(2)}) collective-permute-start(f32[3,2,8,16]{3,2,1,0:T(8,128)S(1)} %get-tuple-element.29), channel_id=1, source_target_pairs={{0,8},{8,16},{16,24},{1,9},{9,17},{17,25},{2,10},{10,18},{18,26},{... | collective-permute-start | bytes 9224 | tf_op jit(solution)/shard_map/ppermute | solution.py:17
  14.0 4.3 %collective-permute-start.13 = (f32[3,2,8,16]{3,2,1,0:T(8,128)S(1)}, f32[3,2,8,16]{3,2,1,0:T(8,128)S(1)}, u32[]{:S(2)}, u32[]{:S(2)}) collective-permute-start(f32[3,2,8,16]{3,2,1,0:T(8,128)S(1)} %get-tuple-element.28), channel_id=1, source_target_pairs={{8,0},{16,8},{24,16},{9,1},{17,9},{25,17},{10,2},{18,10},{26,18},{... | collective-permute-start | bytes 9224 | tf_op jit(solution)/shard_map/ppermute | solution.py:20
  18.3 5.0 %collective-permute-start.14 = (f32[3,12,2,16]{3,2,1,0:T(2,128)S(1)}, f32[3,12,2,16]{3,2,1,0:T(2,128)S(1)}, u32[]{:S(2)}, u32[]{:S(2)}) collective-permute-start(f32[3,12,2,16]{3,2,1,0:T(2,128)S(1)} %get-tuple-element.24), channel_id=1, source_target_pairs={{0,4},{1,5},{2,6},{3,7},{8,12},{9,13},{10,14},{11,15},{16,20},{17,... | collective-permute-start | bytes 13832 | tf_op jit(solution)/shard_map/ppermute | solution.py:17
  21.8 5.9 %collective-permute-start.15 = (f32[3,12,2,16]{3,2,1,0:T(2,128)S(1)}, f32[3,12,2,16]{3,2,1,0:T(2,128)S(1)}, u32[]{:S(2)}, u32[]{:S(2)}) collective-permute-start(f32[3,12,2,16]{3,2,1,0:T(2,128)S(1)} %get-tuple-element.25), channel_id=1, source_target_pairs={{4,0},{5,1},{6,2},{7,3},{12,8},{13,9},{14,10},{15,11},{20,16},{21,... | collective-permute-start | bytes 13832 | tf_op jit(solution)/shard_map/ppermute | solution.py:20
  27.8 10.7 %collective-permute-start.16 = (f32[3,12,12,2]{3,2,1,0:T(8,128)S(1)}, f32[3,12,12,2]{3,2,1,0:T(8,128)S(1)}, u32[]{:S(2)}, u32[]{:S(2)}) collective-permute-start(f32[3,12,12,2]{3,2,1,0:T(8,128)S(1)} %get-tuple-element.20), channel_id=1, source_target_pairs={{0,1},{1,2},{2,3},{4,5},{5,6},{6,7},{8,9},{9,10},{10,11},{12,13},{... | collective-permute-start | bytes 10376 | tf_op jit(solution)/shard_map/ppermute | solution.py:17
  31.3 11.7 %collective-permute-start.17 = (f32[3,12,12,2]{3,2,1,0:T(8,128)S(1)}, f32[3,12,12,2]{3,2,1,0:T(8,128)S(1)}, u32[]{:S(2)}, u32[]{:S(2)}) collective-permute-start(f32[3,12,12,2]{3,2,1,0:T(8,128)S(1)} %get-tuple-element.21), channel_id=1, source_target_pairs={{1,0},{2,1},{3,2},{5,4},{6,5},{7,6},{9,8},{10,9},{11,10},{13,12},{... | collective-permute-start | bytes 10376 | tf_op jit(solution)/shard_map/ppermute | solution.py:20
  44.0 5.1 %collective-permute-start.2 = (f32[68,2,128]{2,1,0:T(2,128)S(1)}, f32[68,2,128]{2,1,0:T(2,128)S(1)}, u32[]{:S(2)}, u32[]{:S(2)}) collective-permute-start(f32[68,2,128]{2,1,0:T(2,128)S(1)} %get-tuple-element.14), channel_id=1, source_target_pairs={{0,4},{1,5},{2,6},{3,7},{8,12},{9,13},{10,14},{11,15},{16,20},{17,... | collective-permute-start | bytes 208904 | tf_op jit(solution)/shard_map/ppermute | solution.py:17
  45.5 6.2 %collective-permute-start.3 = (f32[68,2,128]{2,1,0:T(2,128)S(1)}, f32[68,2,128]{2,1,0:T(2,128)S(1)}, u32[]{:S(2)}, u32[]{:S(2)}) collective-permute-start(f32[68,2,128]{2,1,0:T(2,128)S(1)} %get-tuple-element.15), channel_id=1, source_target_pairs={{4,0},{5,1},{6,2},{7,3},{12,8},{13,9},{14,10},{15,11},{20,16},{21,... | collective-permute-start | bytes 208904 | tf_op jit(solution)/shard_map/ppermute | solution.py:20
  57.7 11.0 %collective-permute-start.5 = (f32[68,68,2]{1,0,2:T(8,128)S(1)}, f32[68,68,2]{1,0,2:T(8,128)S(1)}, u32[]{:S(2)}, u32[]{:S(2)}) collective-permute-start(f32[68,68,2]{1,0,2:T(8,128)S(1)} %copy.19), channel_id=1, source_target_pairs={{1,0},{2,1},{3,2},{5,4},{6,5},{7,6},{9,8},{10,9},{11,10},{13,12},{... | collective-permute-start | bytes 110984 | tf_op jit(solution)/shard_map/ppermute | solution.py:20
  61.6 9.5 %collective-permute-start.4 = (f32[68,68,2]{1,2,0:T(2,128)S(1)}, f32[68,68,2]{1,2,0:T(2,128)S(1)}, u32[]{:S(2)}, u32[]{:S(2)}) collective-permute-start(f32[68,68,2]{1,2,0:T(2,128)S(1)} %copy.17), channel_id=1, source_target_pairs={{0,1},{1,2},{2,3},{4,5},{5,6},{6,7},{8,9},{9,10},{10,11},{12,13},{... | collective-permute-start | bytes 110984 | tf_op jit(solution)/shard_map/ppermute | solution.py:17
  73.5 10.4 %copy-start = (f32[1,64,64,128]{3,2,1,0:T(8,128)S(1)}, f32[1,64,64,128]{3,2,1,0:T(8,128)}, u32[]{:S(2)}) copy-start(f32[1,64,64,128]{3,2,1,0:T(8,128)} %fusion.19) | copy-start | bytes 6291460
  73.5 10.4 %copy-start.1 = (f32[1,64,64,128]{3,2,1,0:T(8,128)S(1)}, f32[1,64,64,128]{3,2,1,0:T(8,128)}, u32[]{:S(2)}) copy-start(f32[1,64,64,128]{3,2,1,0:T(8,128)} %fusion.9) | copy-start | bytes 6291460
  73.5 10.4 %copy-start.2 = (f32[64,64,128]{2,1,0:T(8,128)S(1)}, f32[64,64,128]{2,1,0:T(8,128)}, u32[]{:S(2)}) copy-start(f32[64,64,128]{2,1,0:T(8,128)} %get-tuple-element.8) | copy-start | bytes 6291460
  92.9 9.9 %collective-permute-start.6 = (f32[3,2,12,20]{3,2,1,0:T(8,128)S(1)}, f32[3,2,12,20]{3,2,1,0:T(8,128)S(1)}, u32[]{:S(2)}, u32[]{:S(2)}) collective-permute-start(f32[3,2,12,20]{3,2,1,0:T(8,128)S(1)} %get-tuple-element.18), channel_id=1, source_target_pairs={{0,8},{8,16},{16,24},{1,9},{9,17},{17,25},{2,10},{10,18},{18,26},{... | collective-permute-start | bytes 17288 | tf_op jit(solution)/shard_map/ppermute | solution.py:17
  94.2 8.6 %collective-permute-start.7 = (f32[3,2,12,20]{3,2,1,0:T(8,128)S(1)}, f32[3,2,12,20]{3,2,1,0:T(8,128)S(1)}, u32[]{:S(2)}, u32[]{:S(2)}) collective-permute-start(f32[3,2,12,20]{3,2,1,0:T(8,128)S(1)} %get-tuple-element.19), channel_id=1, source_target_pairs={{8,0},{16,8},{24,16},{9,1},{17,9},{25,17},{10,2},{18,10},{26,18},{... | collective-permute-start | bytes 17288 | tf_op jit(solution)/shard_map/ppermute | solution.py:20
  102.9 46.3 %collective-permute-start.8 = (f32[3,8,2,20]{3,2,1,0:T(2,128)S(1)}, f32[3,8,2,20]{3,2,1,0:T(2,128)S(1)}, u32[]{:S(2)}, u32[]{:S(2)}) collective-permute-start(f32[3,8,2,20]{3,2,1,0:T(2,128)S(1)} %get-tuple-element.22), channel_id=1, source_target_pairs={{0,4},{1,5},{2,6},{3,7},{8,12},{9,13},{10,14},{11,15},{16,20},{17,... | collective-permute-start | bytes 11528 | tf_op jit(solution)/shard_map/ppermute | solution.py:17
  104.7 44.5 %collective-permute-start.9 = (f32[3,8,2,20]{3,2,1,0:T(2,128)S(1)}, f32[3,8,2,20]{3,2,1,0:T(2,128)S(1)}, u32[]{:S(2)}, u32[]{:S(2)}) collective-permute-start(f32[3,8,2,20]{3,2,1,0:T(2,128)S(1)} %get-tuple-element.23), channel_id=1, source_target_pairs={{4,0},{5,1},{6,2},{7,3},{12,8},{13,9},{14,10},{15,11},{20,16},{21,... | collective-permute-start | bytes 11528 | tf_op jit(solution)/shard_map/ppermute | solution.py:20
  149.3 4.4 %collective-permute-start.10 = (f32[3,8,8,2]{3,2,1,0:T(8,128)S(1)}, f32[3,8,8,2]{3,2,1,0:T(8,128)S(1)}, u32[]{:S(2)}, u32[]{:S(2)}) collective-permute-start(f32[3,8,8,2]{3,2,1,0:T(8,128)S(1)} %get-tuple-element.26), channel_id=1, source_target_pairs={{0,1},{1,2},{2,3},{4,5},{5,6},{6,7},{8,9},{9,10},{10,11},{12,13},{... | collective-permute-start | bytes 4616 | tf_op jit(solution)/shard_map/ppermute | solution.py:17
  151.5 6.5 %collective-permute-start.11 = (f32[3,8,8,2]{3,2,1,0:T(8,128)S(1)}, f32[3,8,8,2]{3,2,1,0:T(8,128)S(1)}, u32[]{:S(2)}, u32[]{:S(2)}) collective-permute-start(f32[3,8,8,2]{3,2,1,0:T(8,128)S(1)} %get-tuple-element.27), channel_id=1, source_target_pairs={{1,0},{2,1},{3,2},{5,4},{6,5},{7,6},{9,8},{10,9},{11,10},{13,12},{... | collective-permute-start | bytes 4616 | tf_op jit(solution)/shard_map/ppermute | solution.py:20
where the time goes:
time: 160 us; the launch traced here: 159 us
  blocking collectives  42.9 us (27%)
  starting transfers between devices  37.7 us (24%)
  waiting for transfers between devices  24.6 us (15%)
  other arithmetic  23.4 us (15%)
  matrix products  15.2 us (10%)
  local copies, waits for them, and re-layouts  13.9 us (9%)
    psum x1, blocking collectives, per_device(): coarse_sum = lax.psum(coarse_part, ('gx', 'gy', 'gz'))  42.9 us
    ppermute x9, starting transfers between devices, padded_2(): lax.ppermute(lax.slice_in_dim(block, block.shape[dim] - width, None, axis...  25.9 us
    ppermute x9, waiting for transfers between devices, padded_2(): lax.ppermute(lax.slice_in_dim(block, 0, width, axis=dim), axis, backward)  18.3 us
    another operation x3, other arithmetic, per_device(): force = jnp.stack(slopes) * difference[None]  14.7 us
    dot_general x2, matrix products, project(): section = jnp.einsum('axyz,xp->apyz', force, along_x, precision=highest)  13 us
    ppermute x9, starting transfers between devices, padded_2(): lax.ppermute(lax.slice_in_dim(block, 0, width, axis=dim), axis, backward)  11.9 us
    ppermute x9, waiting for transfers between devices, padded_2(): lax.ppermute(lax.slice_in_dim(block, block.shape[dim] - width, None, axis...  6.36 us
    slice x8, local copies, waits for them, and re-layouts, padded_2(): lax.slice_in_dim(block, block.shape[dim] - width, None, axis=dim)  5.86 us
  transfers between devices with their start and end apart: 18, of which 8 were waited for; matrix products, arithmetic and copies ran while one was open for 12% of the time, Pallas kernels for 0%

commit v1 on v0

--- a/solution.py
+++ b/solution.py
@@ -116,7 +116,7 @@
     coarse_y = basis_matrix(size_y, coarse_control.shape[2], SPC, lax.axis_index("gy") * size_y, 0)
     coarse_z = basis_matrix(size_z, coarse_control.shape[3], SPC, lax.axis_index("gz") * size_z, 0)
     coarse_part = project(force, coarse_x, coarse_y, coarse_z)
-    coarse_sum = lax.psum(coarse_part, ("gx", "gy", "gz"))
+    coarse_sum = jnp.sum(lax.all_gather(coarse_part, ("gx", "gy", "gz")), axis=0)
     coarse_gradient = coarse_sum * SPC ** (-1.5) + bend_factor * laplace(laplace(coarse_control))
     return (fine_gradient, coarse_gradient)
 

time: 160 us -> 200 us (1.25)
  blocking collectives: 42.9 us -> 83.2 us
    all_gather x0 -> x1, blocking collectives: none -> 83.2 us  [per_device(): lax.all_gather(coarse_part, ('gx', 'gy', 'gz'))]
    psum x1 -> x0, blocking collectives: 42.9 us -> none  [per_device(): coarse_sum = lax.psum(coarse_part, ('gx', 'gy', 'gz'))]
  transfers between devices with their start and end apart: 18 -> 18, of which waited for: 8 -> 8; matrix products, arithmetic and copies ran while one was open for 12% -> 10% of each run, Pallas kernels for 0% -> 0%
where the time goes in v1:
time: 200 us; the launch traced here: 199 us
  blocking collectives  83.2 us (42%)
  starting transfers between devices  37.9 us (19%)
  waiting for transfers between devices  24.7 us (12%)
  other arithmetic  23.4 us (12%)
  matrix products  15.3 us (8%)
  local copies, waits for them, and re-layouts  13.9 us (7%)
    all_gather x1, blocking collectives, per_device(): lax.all_gather(coarse_part, ('gx', 'gy', 'gz'))  83.2 us
    ppermute x9, starting transfers between devices, padded_2(): lax.ppermute(lax.slice_in_dim(block, block.shape[dim] - width, None, axis...  26 us
    ppermute x9, waiting for transfers between devices, padded_2(): lax.ppermute(lax.slice_in_dim(block, 0, width, axis=dim), axis, backward)  18.3 us
    another operation x3, other arithmetic, per_device(): force = jnp.stack(slopes) * difference[None]  14.7 us
    dot_general x2, matrix products, project(): section = jnp.einsum('axyz,xp->apyz', force, along_x, precision=highest)  13 us
    ppermute x9, starting transfers between devices, padded_2(): lax.ppermute(lax.slice_in_dim(block, 0, width, axis=dim), axis, backward)  11.9 us
    ppermute x9, waiting for transfers between devices, padded_2(): lax.ppermute(lax.slice_in_dim(block, block.shape[dim] - width, None, axis...  6.36 us
    slice x8, local copies, waits for them, and re-layouts, padded_2(): lax.slice_in_dim(block, block.shape[dim] - width, None, axis=dim)  5.86 us
  transfers between devices with their start and end apart: 18, of which 8 were waited for; matrix products, arithmetic and copies ran while one was open for 10% of the time, Pallas kernels for 0%

profile of v1, /device:TPU:0, one launch (start us, length us, event | category | flops | bytes accessed | tf_op | source)
XLA Modules:
  0.0 199.4 jit_solution(1244088295266833155)
XLA Ops:
  0.7 4.2 %fusion.237 = (f32[64,64,128]{2,1,0:T(8,128)}, f32[64,64,128]{2,1,0:T(8,128)S(1)}) fusion(f32[64,64,128]{2,1,0:T(8,128)} %param.4, f32[64,64,128]{2,1,0:T(8,128)} %param.5), kind=kLoop, calls=%fused_computation.303 | loop fusion | flops 1048576 | bytes 8388608 | tf_op jit(solution)/shard_map/sub | solution.py:91
  4.9 2.4 %collective-permute-start = (f32[2,64,128]{2,1,0:T(8,128)S(1)}, f32[2,64,128]{2,1,0:T(8,128)S(1)}, u32[]{:S(2)}, u32[]{:S(2)}) collective-permute-start(f32[2,64,128]{2,1,0:T(8,128)S(1)} %get-tuple-element.14), channel_id=1, source_target_pairs={{0,8},{8,16},{16,24},{1,9},{9,17},{17,25},{2,10},{10,18},{18,26},{... | collective-permute-start | bytes 196616 | tf_op jit(solution)/shard_map/ppermute | solution.py:17
  7.3 1.3 collective-permute-start.1
  8.6 5.1 %collective-permute-start.12 = (f32[3,2,8,16]{3,2,1,0:T(8,128)S(1)}, f32[3,2,8,16]{3,2,1,0:T(8,128)S(1)}, u32[]{:S(2)}, u32[]{:S(2)}) collective-permute-start(f32[3,2,8,16]{3,2,1,0:T(8,128)S(1)} %get-tuple-element.27), channel_id=1, source_target_pairs={{0,8},{8,16},{16,24},{1,9},{9,17},{17,25},{2,10},{10,18},{18,26},{... | collective-permute-start | bytes 9224 | tf_op jit(solution)/shard_map/ppermute | solution.py:17
  13.8 1.3 collective-permute-start.13
  15.2 0.1 fusion.51
  15.3 0.1 broadcast_multiply_fusion.1
  15.4 0.1 broadcast_multiply_fusion
  15.5 0.0 collective-permute-done.12
  15.5 2.6 %collective-permute-done.13 = f32[3,2,8,16]{3,2,1,0:T(8,128)S(1)} collective-permute-done((f32[3,2,8,16]{3,2,1,0:T(8,128)S(1)}, f32[3,2,8,16]{3,2,1,0:T(8,128)S(1)}, u32[]{:S(2)}, u32[]{:S(2)}) %collective-permute-start.13) | collective-permute-done | bytes 3104 | tf_op jit(solution)/shard_map/ppermute | solution.py:20
  18.1 3.4 %collective-permute-start.14 = (f32[3,12,2,16]{3,2,1,0:T(2,128)S(1)}, f32[3,12,2,16]{3,2,1,0:T(2,128)S(1)}, u32[]{:S(2)}, u32[]{:S(2)}) collective-permute-start(f32[3,12,2,16]{3,2,1,0:T(2,128)S(1)} %get-tuple-element.22), channel_id=1, source_target_pairs={{0,4},{1,5},{2,6},{3,7},{8,12},{9,13},{10,14},{11,15},{16,20},{17,... | collective-permute-start | bytes 13832 | tf_op jit(solution)/shard_map/ppermute | solution.py:17
  21.6 1.3 collective-permute-start.15
  22.9 0.3 collective-permute-done.14
  23.2 4.2 %collective-permute-done.15 = f32[3,12,2,16]{3,2,1,0:T(2,128)S(1)} collective-permute-done((f32[3,12,2,16]{3,2,1,0:T(2,128)S(1)}, f32[3,12,2,16]{3,2,1,0:T(2,128)S(1)}, u32[]{:S(2)}, u32[]{:S(2)}) %collective-permute-start.15) | collective-permute-done | bytes 4640 | tf_op jit(solution)/shard_map/ppermute | solution.py:20
  27.4 0.1 pad_maximum_fusion.14
  27.5 0.1 fusion.241
  27.6 3.5 %collective-permute-start.16 = (f32[3,12,12,2]{3,2,1,0:T(8,128)S(1)}, f32[3,12,12,2]{3,2,1,0:T(8,128)S(1)}, u32[]{:S(2)}, u32[]{:S(2)}) collective-permute-start(f32[3,12,12,2]{3,2,1,0:T(8,128)S(1)} %get-tuple-element.18), channel_id=1, source_target_pairs={{0,1},{1,2},{2,3},{4,5},{5,6},{6,7},{8,9},{9,10},{10,11},{12,13},{... | collective-permute-start | bytes 10376 | tf_op jit(solution)/shard_map/ppermute | solution.py:17
  31.1 1.3 collective-permute-start.17
  32.5 5.9 %collective-permute-done.16 = f32[3,12,12,2]{3,2,1,0:T(8,128)S(1)} collective-permute-done((f32[3,12,12,2]{3,2,1,0:T(8,128)S(1)}, f32[3,12,12,2]{3,2,1,0:T(8,128)S(1)}, u32[]{:S(2)}, u32[]{:S(2)}) %collective-permute-start.16) | collective-permute-done | bytes 3488 | tf_op jit(solution)/shard_map/ppermute | solution.py:17
  38.3 4.4 %collective-permute-done.17 = f32[3,12,12,2]{3,2,1,0:T(8,128)S(1)} collective-permute-done((f32[3,12,12,2]{3,2,1,0:T(8,128)S(1)}, f32[3,12,12,2]{3,2,1,0:T(8,128)S(1)}, u32[]{:S(2)}, u32[]{:S(2)}) %collective-permute-start.17) | collective-permute-done | bytes 3488 | tf_op jit(solution)/shard_map/ppermute | solution.py:20
  42.8 0.3 pad_maximum_fusion.15
  43.1 0.6 fusion.36
  43.7 0.0 collective-permute-done
  43.7 0.1 pad_maximum_fusion.24
  43.8 1.6 collective-permute-start.2
  45.3 1.3 collective-permute-start.3
  46.6 2.2 %fusion.9 = f32[1,64,64,128]{3,2,1,0:T(8,128)} fusion(f32[64,64,128]{2,1,0:T(8,128)S(1)} %get-tuple-element.7, f32[2,64,128]{2,1,0:T(8,128)S(1)} %collective-permute-done.1, f32[2,64,128]{2,1,0:T(8,128)S(1)} %collective-permute-done), kind=kLoop, calls=%fused_computation.17 | loop fusion | flops 5242880 | bytes 4325376 | tf_op jit(solution)/shard_map/stack | solution.py:94
  48.8 0.0 collective-permute-done.2
  48.8 2.7 %collective-permute-done.3 = f32[68,2,128]{2,1,0:T(2,128)S(1)} collective-permute-done((f32[68,2,128]{2,1,0:T(2,128)S(1)}, f32[68,2,128]{2,1,0:T(2,128)S(1)}, u32[]{:S(2)}, u32[]{:S(2)}) %collective-permute-start.3) | collective-permute-done | bytes 69664 | tf_op jit(solution)/shard_map/ppermute | solution.py:20
  51.5 0.4 pad_maximum_fusion.1
  51.9 3.0 %fusion.238 = (f32[68,68,2]{2,1,0:T(8,128)}, f32[68,68,2]{2,1,0:T(8,128)}) fusion(f32[68,68,128]{2,1,0:T(8,128)S(1)} %pad_maximum_fusion.1), kind=kLoop, calls=%fused_computation.304 | loop fusion | bytes 147968 | tf_op jit(solution)/shard_map/slice | solution.py:18
  54.9 2.6 %copy.16 = f32[68,68,2]{1,0,2:T(8,128)S(1)} copy(f32[68,68,2]{2,1,0:T(8,128)} %get-tuple-element.9) | data formatting | bytes 73984 | tf_op jit(solution)/shard_map/slice | solution.py:20
  57.5 1.3 collective-permute-start.5
  58.8 2.6 %copy.14 = f32[68,68,2]{1,2,0:T(2,128)S(1)} copy(f32[68,68,2]{2,1,0:T(8,128)} %get-tuple-element.8) | data formatting | bytes 73984 | tf_op jit(solution)/shard_map/slice | solution.py:18
  61.4 4.6 %collective-permute-start.4 = (f32[68,68,2]{1,2,0:T(2,128)S(1)}, f32[68,68,2]{1,2,0:T(2,128)S(1)}, u32[]{:S(2)}, u32[]{:S(2)}) collective-permute-start(f32[68,68,2]{1,2,0:T(2,128)S(1)} %copy.14), channel_id=1, source_target_pairs={{0,1},{1,2},{2,3},{4,5},{5,6},{6,7},{8,9},{9,10},{10,11},{12,13},{... | collective-permute-start | bytes 110984 | tf_op jit(solution)/shard_map/ppermute | solution.py:17
  66.0 0.4 maximum_maximum_fusion
  66.4 2.1 %fusion.19 = f32[1,64,64,128]{3,2,1,0:T(8,128)} fusion(f32[68,66,128]{2,1,0:T(8,128)S(1)} %get-tuple-element.11, f32[68,66,128]{2,1,0:T(8,128)S(1)} %get-tuple-element.10), kind=kLoop, calls=%fused_computation.39 | loop fusion | flops 3145728 | bytes 10485760 | tf_op jit(solution)/shard_map/stack | solution.py:94
  68.6 0.0 collective-permute-done.5
  68.6 2.4 %copy.17 = f32[68,68,2]{2,1,0:T(8,128)} copy(f32[68,68,2]{1,0,2:T(8,128)S(1)} %collective-permute-done.5) | data formatting | bytes 73984 | tf_op jit(solution)/shard_map/ppermute | solution.py:20
  70.9 2.4 %copy.15 = f32[68,68,2]{2,1,0:T(8,128)} copy(f32[68,68,2]{1,2,0:T(2,128)S(1)} %collective-permute-done.4) | data formatting | bytes 73984 | tf_op jit(solution)/shard_map/ppermute | solution.py:17
  73.3 10.4 %fusion.14 = f32[1,64,64,128]{3,2,1,0:T(8,128)S(1)} fusion(f32[68,68,2]{2,1,0:T(8,128)} %copy.17, f32[68,2,128]{2,1,0:T(2,128)S(1)} %collective-permute-done.3, f32[68,2,128]{2,1,0:T(2,128)S(1)} %collective-permute-done.2, f32[2,64,128]{2,1,0:T(8,128)S(1)} %collective-permute-done.1, f32[64,64,128]{2,1,0:T(8,128)S(1)} %get-tuple-element.7, ...), kind=kLoop, calls=%fused_computation.23 | loop fusion | flops 13631488 | bytes 4538624 | tf_op jit(solution)/shard_map/stack | solution.py:94
  83.7 1.1 maximum_multiply_fusion
  84.8 6.5 %fusion.23 = f32[3,12,64,128]{3,1,2,0:T(8,128)S(1)} fusion(f32[3,64,64,128]{3,2,1,0:T(8,128)S(1)} %maximum_multiply_fusion, f32[12]{0:T(128)S(1)} %multiply_add_fusion.4, f32[64]{0:T(128)S(1)} %convert_add_fusion.4), kind=kOutput, calls=%fused_computation.47 | convolution fusion | flops 226506240 | bytes 7471408 | tf_op jit(solution)/shard_map/axyz,xp->apyz/dot_general | solution.py:68
  91.3 1.0 fusion.31
  92.3 0.5 fusion.65
  92.8 1.3 collective-permute-start.6
  94.1 1.5 collective-permute-start.7
  95.6 6.5 %fusion.26 = f32[3,8,64,128]{3,1,2,0:T(8,128)S(1)} fusion(f32[3,64,64,128]{3,2,1,0:T(8,128)S(1)} %maximum_multiply_fusion, f32[8]{0:T(128)S(1)} %multiply_add_fusion.1, f32[64]{0:T(128)S(1)} %convert_add_fusion.1), kind=kOutput, calls=%fused_computation.48 | convolution fusion | flops 151004160 | bytes 7078176 | tf_op jit(solution)/shard_map/axyz,xp->apyz/dot_general | solution.py:68
  102.1 0.6 convolution_bitcast_fusion
  102.6 0.3 fusion.60
  102.9 0.0 collective-permute-done.6
  103.0 1.8 collective-permute-start.8
  104.8 1.3 collective-permute-start.9
  106.1 83.2 %all-gather = f32[96,8,4,16]{3,1,2,0:T(8,128)S(1)} all-gather(f32[3,8,4,16]{3,1,2,0:T(8,128)S(1)} %fusion.60), channel_id=2, replica_groups=mesh['gx'=4,'gy'=2,'gz'=4] {'gx','gy','gz'}, dimensions={0}, use_global_device_ids=true | all-gather | bytes 202752 | tf_op jit(solution)/shard_map/all_gather | solution.py:119
  189.3 0.2 reduce_sum.9
  189.5 0.0 collective-permute-done.8
  189.5 0.1 fusion.244
  189.6 2.4 %collective-permute-start.10 = (f32[3,8,8,2]{3,2,1,0:T(8,128)S(1)}, f32[3,8,8,2]{3,2,1,0:T(8,128)S(1)}, u32[]{:S(2)}, u32[]{:S(2)}) collective-permute-start(f32[3,8,8,2]{3,2,1,0:T(8,128)S(1)} %get-tuple-element.24), channel_id=1, source_target_pairs={{0,1},{1,2},{2,3},{4,5},{5,6},{6,7},{8,9},{9,10},{10,11},{12,13},{... | collective-permute-start | bytes 4616 | tf_op jit(solution)/shard_map/ppermute | solution.py:17
  192.0 1.3 collective-permute-start.11
  193.3 0.1 fusion.59
  193.4 0.6 copy.25
  194.0 0.2 collective-permute-done.10
  194.2 4.3 %collective-permute-done.11 = f32[3,8,8,2]{3,2,1,0:T(8,128)S(1)} collective-permute-done((f32[3,8,8,2]{3,2,1,0:T(8,128)S(1)}, f32[3,8,8,2]{3,2,1,0:T(8,128)S(1)}, u32[]{:S(2)}, u32[]{:S(2)}) %collective-permute-start.11) | collective-permute-done | bytes 1568 | tf_op jit(solution)/shard_map/ppermute | solution.py:20
  198.5 0.9 fusion.42
  (37 shorter events, 0.3 us)
Async XLA Ops:
  0.6 8.0 %copy-start.3 = (f32[3,8,8,16]{3,2,1,0:T(8,128)S(1)}, f32[3,8,8,16]{3,2,1,0:T(8,128)}, u32[]{:S(2)}) copy-start(f32[3,8,8,16]{3,2,1,0:T(8,128)} %param.6) | copy-start | bytes 36868
  0.6 14.5 %copy-start.4 = (f32[3,8,4,16]{3,2,1,0:T(4,128)S(1)}, f32[3,8,4,16]{3,2,1,0:T(4,128)}, u32[]{:S(2)}) copy-start(f32[3,8,4,16]{3,2,1,0:T(4,128)} %param.7) | copy-start | bytes 18436
  4.9 38.8 %collective-permute-start = (f32[2,64,128]{2,1,0:T(8,128)S(1)}, f32[2,64,128]{2,1,0:T(8,128)S(1)}, u32[]{:S(2)}, u32[]{:S(2)}) collective-permute-start(f32[2,64,128]{2,1,0:T(8,128)S(1)} %get-tuple-element.14), channel_id=1, source_target_pairs={{0,8},{8,16},{16,24},{1,9},{9,17},{17,25},{2,10},{10,18},{18,26},{... | collective-permute-start | bytes 196616 | tf_op jit(solution)/shard_map/ppermute | solution.py:17
  7.3 36.4 %collective-permute-start.1 = (f32[2,64,128]{2,1,0:T(8,128)S(1)}, f32[2,64,128]{2,1,0:T(8,128)S(1)}, u32[]{:S(2)}, u32[]{:S(2)}) collective-permute-start(f32[2,64,128]{2,1,0:T(8,128)S(1)} %get-tuple-element.15), channel_id=1, source_target_pairs={{8,0},{16,8},{24,16},{9,1},{17,9},{25,17},{10,2},{18,10},{26,18},{... | collective-permute-start | bytes 196616 | tf_op jit(solution)/shard_map/ppermute | solution.py:20
  8.6 6.9 %collective-permute-start.12 = (f32[3,2,8,16]{3,2,1,0:T(8,128)S(1)}, f32[3,2,8,16]{3,2,1,0:T(8,128)S(1)}, u32[]{:S(2)}, u32[]{:S(2)}) collective-permute-start(f32[3,2,8,16]{3,2,1,0:T(8,128)S(1)} %get-tuple-element.27), channel_id=1, source_target_pairs={{0,8},{8,16},{16,24},{1,9},{9,17},{17,25},{2,10},{10,18},{18,26},{... | collective-permute-start | bytes 9224 | tf_op jit(solution)/shard_map/ppermute | solution.py:17
  13.8 4.3 %collective-permute-start.13 = (f32[3,2,8,16]{3,2,1,0:T(8,128)S(1)}, f32[3,2,8,16]{3,2,1,0:T(8,128)S(1)}, u32[]{:S(2)}, u32[]{:S(2)}) collective-permute-start(f32[3,2,8,16]{3,2,1,0:T(8,128)S(1)} %get-tuple-element.26), channel_id=1, source_target_pairs={{8,0},{16,8},{24,16},{9,1},{17,9},{25,17},{10,2},{18,10},{26,18},{... | collective-permute-start | bytes 9224 | tf_op jit(solution)/shard_map/ppermute | solution.py:20
  18.1 5.0 %collective-permute-start.14 = (f32[3,12,2,16]{3,2,1,0:T(2,128)S(1)}, f32[3,12,2,16]{3,2,1,0:T(2,128)S(1)}, u32[]{:S(2)}, u32[]{:S(2)}) collective-permute-start(f32[3,12,2,16]{3,2,1,0:T(2,128)S(1)} %get-tuple-element.22), channel_id=1, source_target_pairs={{0,4},{1,5},{2,6},{3,7},{8,12},{9,13},{10,14},{11,15},{16,20},{17,... | collective-permute-start | bytes 13832 | tf_op jit(solution)/shard_map/ppermute | solution.py:17
  21.6 5.9 %collective-permute-start.15 = (f32[3,12,2,16]{3,2,1,0:T(2,128)S(1)}, f32[3,12,2,16]{3,2,1,0:T(2,128)S(1)}, u32[]{:S(2)}, u32[]{:S(2)}) collective-permute-start(f32[3,12,2,16]{3,2,1,0:T(2,128)S(1)} %get-tuple-element.23), channel_id=1, source_target_pairs={{4,0},{5,1},{6,2},{7,3},{12,8},{13,9},{14,10},{15,11},{20,16},{21,... | collective-permute-start | bytes 13832 | tf_op jit(solution)/shard_map/ppermute | solution.py:20
  27.6 10.7 %collective-permute-start.16 = (f32[3,12,12,2]{3,2,1,0:T(8,128)S(1)}, f32[3,12,12,2]{3,2,1,0:T(8,128)S(1)}, u32[]{:S(2)}, u32[]{:S(2)}) collective-permute-start(f32[3,12,12,2]{3,2,1,0:T(8,128)S(1)} %get-tuple-element.18), channel_id=1, source_target_pairs={{0,1},{1,2},{2,3},{4,5},{5,6},{6,7},{8,9},{9,10},{10,11},{12,13},{... | collective-permute-start | bytes 10376 | tf_op jit(solution)/shard_map/ppermute | solution.py:17
  31.1 11.7 %collective-permute-start.17 = (f32[3,12,12,2]{3,2,1,0:T(8,128)S(1)}, f32[3,12,12,2]{3,2,1,0:T(8,128)S(1)}, u32[]{:S(2)}, u32[]{:S(2)}) collective-permute-start(f32[3,12,12,2]{3,2,1,0:T(8,128)S(1)} %get-tuple-element.19), channel_id=1, source_target_pairs={{1,0},{2,1},{3,2},{5,4},{6,5},{7,6},{9,8},{10,9},{11,10},{13,12},{... | collective-permute-start | bytes 10376 | tf_op jit(solution)/shard_map/ppermute | solution.py:20
  43.8 5.0 %collective-permute-start.2 = (f32[68,2,128]{2,1,0:T(2,128)S(1)}, f32[68,2,128]{2,1,0:T(2,128)S(1)}, u32[]{:S(2)}, u32[]{:S(2)}) collective-permute-start(f32[68,2,128]{2,1,0:T(2,128)S(1)} %get-tuple-element.12), channel_id=1, source_target_pairs={{0,4},{1,5},{2,6},{3,7},{8,12},{9,13},{10,14},{11,15},{16,20},{17,... | collective-permute-start | bytes 208904 | tf_op jit(solution)/shard_map/ppermute | solution.py:17
  45.3 6.2 %collective-permute-start.3 = (f32[68,2,128]{2,1,0:T(2,128)S(1)}, f32[68,2,128]{2,1,0:T(2,128)S(1)}, u32[]{:S(2)}, u32[]{:S(2)}) collective-permute-start(f32[68,2,128]{2,1,0:T(2,128)S(1)} %get-tuple-element.13), channel_id=1, source_target_pairs={{4,0},{5,1},{6,2},{7,3},{12,8},{13,9},{14,10},{15,11},{20,16},{21,... | collective-permute-start | bytes 208904 | tf_op jit(solution)/shard_map/ppermute | solution.py:20
  57.5 11.0 %collective-permute-start.5 = (f32[68,68,2]{1,0,2:T(8,128)S(1)}, f32[68,68,2]{1,0,2:T(8,128)S(1)}, u32[]{:S(2)}, u32[]{:S(2)}) collective-permute-start(f32[68,68,2]{1,0,2:T(8,128)S(1)} %copy.16), channel_id=1, source_target_pairs={{1,0},{2,1},{3,2},{5,4},{6,5},{7,6},{9,8},{10,9},{11,10},{13,12},{... | collective-permute-start | bytes 110984 | tf_op jit(solution)/shard_map/ppermute | solution.py:20
  61.4 9.5 %collective-permute-start.4 = (f32[68,68,2]{1,2,0:T(2,128)S(1)}, f32[68,68,2]{1,2,0:T(2,128)S(1)}, u32[]{:S(2)}, u32[]{:S(2)}) collective-permute-start(f32[68,68,2]{1,2,0:T(2,128)S(1)} %copy.14), channel_id=1, source_target_pairs={{0,1},{1,2},{2,3},{4,5},{5,6},{6,7},{8,9},{9,10},{10,11},{12,13},{... | collective-permute-start | bytes 110984 | tf_op jit(solution)/shard_map/ppermute | solution.py:17
  73.3 10.4 %copy-start = (f32[1,64,64,128]{3,2,1,0:T(8,128)S(1)}, f32[1,64,64,128]{3,2,1,0:T(8,128)}, u32[]{:S(2)}) copy-start(f32[1,64,64,128]{3,2,1,0:T(8,128)} %fusion.19) | copy-start | bytes 6291460
  73.3 10.4 %copy-start.1 = (f32[1,64,64,128]{3,2,1,0:T(8,128)S(1)}, f32[1,64,64,128]{3,2,1,0:T(8,128)}, u32[]{:S(2)}) copy-start(f32[1,64,64,128]{3,2,1,0:T(8,128)} %fusion.9) | copy-start | bytes 6291460
  73.3 10.4 %copy-start.2 = (f32[64,64,128]{2,1,0:T(8,128)S(1)}, f32[64,64,128]{2,1,0:T(8,128)}, u32[]{:S(2)}) copy-start(f32[64,64,128]{2,1,0:T(8,128)} %get-tuple-element.6) | copy-start | bytes 6291460
  92.8 10.1 %collective-permute-start.6 = (f32[3,2,12,20]{3,2,1,0:T(8,128)S(1)}, f32[3,2,12,20]{3,2,1,0:T(8,128)S(1)}, u32[]{:S(2)}, u32[]{:S(2)}) collective-permute-start(f32[3,2,12,20]{3,2,1,0:T(8,128)S(1)} %get-tuple-element.16), channel_id=1, source_target_pairs={{0,8},{8,16},{16,24},{1,9},{9,17},{17,25},{2,10},{10,18},{18,26},{... | collective-permute-start | bytes 17288 | tf_op jit(solution)/shard_map/ppermute | solution.py:17
  94.1 8.9 %collective-permute-start.7 = (f32[3,2,12,20]{3,2,1,0:T(8,128)S(1)}, f32[3,2,12,20]{3,2,1,0:T(8,128)S(1)}, u32[]{:S(2)}, u32[]{:S(2)}) collective-permute-start(f32[3,2,12,20]{3,2,1,0:T(8,128)S(1)} %get-tuple-element.17), channel_id=1, source_target_pairs={{8,0},{16,8},{24,16},{9,1},{17,9},{25,17},{10,2},{18,10},{26,18},{... | collective-permute-start | bytes 17288 | tf_op jit(solution)/shard_map/ppermute | solution.py:20
  103.0 86.5 %collective-permute-start.8 = (f32[3,8,2,20]{3,2,1,0:T(2,128)S(1)}, f32[3,8,2,20]{3,2,1,0:T(2,128)S(1)}, u32[]{:S(2)}, u32[]{:S(2)}) collective-permute-start(f32[3,8,2,20]{3,2,1,0:T(2,128)S(1)} %get-tuple-element.20), channel_id=1, source_target_pairs={{0,4},{1,5},{2,6},{3,7},{8,12},{9,13},{10,14},{11,15},{16,20},{17,... | collective-permute-start | bytes 11528 | tf_op jit(solution)/shard_map/ppermute | solution.py:17
  104.8 84.7 %collective-permute-start.9 = (f32[3,8,2,20]{3,2,1,0:T(2,128)S(1)}, f32[3,8,2,20]{3,2,1,0:T(2,128)S(1)}, u32[]{:S(2)}, u32[]{:S(2)}) collective-permute-start(f32[3,8,2,20]{3,2,1,0:T(2,128)S(1)} %get-tuple-element.21), channel_id=1, source_target_pairs={{4,0},{5,1},{6,2},{7,3},{12,8},{13,9},{14,10},{15,11},{20,16},{21,... | collective-permute-start | bytes 11528 | tf_op jit(solution)/shard_map/ppermute | solution.py:20
  189.6 4.6 %collective-permute-start.10 = (f32[3,8,8,2]{3,2,1,0:T(8,128)S(1)}, f32[3,8,8,2]{3,2,1,0:T(8,128)S(1)}, u32[]{:S(2)}, u32[]{:S(2)}) collective-permute-start(f32[3,8,8,2]{3,2,1,0:T(8,128)S(1)} %get-tuple-element.24), channel_id=1, source_target_pairs={{0,1},{1,2},{2,3},{4,5},{5,6},{6,7},{8,9},{9,10},{10,11},{12,13},{... | collective-permute-start | bytes 4616 | tf_op jit(solution)/shard_map/ppermute | solution.py:17
  192.0 6.5 %collective-permute-start.11 = (f32[3,8,8,2]{3,2,1,0:T(8,128)S(1)}, f32[3,8,8,2]{3,2,1,0:T(8,128)S(1)}, u32[]{:S(2)}, u32[]{:S(2)}) collective-permute-start(f32[3,8,8,2]{3,2,1,0:T(8,128)S(1)} %get-tuple-element.25), channel_id=1, source_target_pairs={{1,0},{2,1},{3,2},{5,4},{6,5},{7,6},{9,8},{10,9},{11,10},{13,12},{... | collective-permute-start | bytes 4616 | tf_op jit(solution)/shard_map/ppermute | solution.py:20
